TPU v7x, 512 devices: a 4x2x32 block of a 4x8x32 slice. The times are simulated.
512 devices in a mesh: parts: 2 (over y), seq: 32 (over z), tp: 8 (over x, core).
Axes of the slice: x: 4, y: 2, z: 32, core: 2. Of those that a mesh axis runs over, the one named last changes fastest.
The devices are a block of a 4x8x32 slice.
Arguments:
- tokens: bfloat16 [16384, 8192], P(('parts', 'seq'), 'tp'), parts along dimension 0, may hold values from -6 to 6
- norm_gain: bfloat16 [8192], P('tp'), may hold values from 0.099609375 to 1.8984375
- w_query: bfloat16 [8192, 4096], P('seq', 'tp'), may hold values from -0.0625 to 0.0625
- w_kv: bfloat16 [8192, 2, 1024], P('seq', None, 'tp'), may hold values from -0.0625 to 0.0625
- b_query: float32 [4096], P('tp'), may hold values from -4 to 4
- b_kv: float32 [2, 1024], P(None, 'tp'), may hold values from -4 to 4
- kv_pool: bfloat16 [8192, 2, 8, 1024], P(('parts', 'seq'), None, None, 'tp'), parts along dimension 0, may hold values from -68 to 68
- prefix_pages: int32 [128, 32], P('parts'), parts along dimension 0, may hold values from 0 to 4095, as said below
- prefix_len: int32 [128], P('parts'), parts along dimension 0, may hold values from 0 to 256
- suffix_len: int32 [128], P('parts'), parts along dimension 0, may hold values from 1 to 128
- fresh_owner: int32 [2048, 1], P('parts'), parts along dimension 0, may hold values from 0 to 31; in each aligned block of 32 rows (0 to 31, 32 to 63, ...) at most 2 rows name the same one
Outputs:
- attn_out: bfloat16 [16384, 4096], P(('parts', 'seq'), 'tp'), parts along dimension 0
- fresh_pages: bfloat16 [4096, 2, 8, 1024], P(('parts', 'seq'), None, None, 'tp'), parts along dimension 0
There are 2 independent parts, one for each index of `parts`. A program takes and returns all parts, laid end to end along the dimension named above; an argument that names none is the same for every part. Nothing has to cross between parts.
Inputs may be any that keep to these rules, and one draw needn't show every extreme that they name: `prefix_pages`: page id q lies in the 128 pages of sequence group q // 128. Among the 64 entries of requests 2*g to 2*(g+1)-1, no group holds more than 3, and in every such block some group holds exactly 3. Entries past the matched prefix still name pages. `fresh_owner`: in the rows of one sequence group's requests (aligned blocks of 32 rows) no group is named more than 2 times; some blocks name one exactly 2 times.
All inputs are finite; a program needn't handle non-finite values.
Results may differ from a plain program's by a relative error of at most 0.005.
The roundings to bfloat16 on the way count: a program that leaves them out, or rounds other values in their place, can miss the bound.
Values may be sent and summed in bfloat16 or wider, within the bound.
No kernel may reach another device: no remote copies, remote signals or barrier semaphores. Data moves between devices by JAX's collectives and lax.ppermute only.
A program may use at most 64 MiB of HBM per device.

v0:
```python
import math

import jax
import jax.numpy as jnp
from jax import lax
from jax.sharding import PartitionSpec as P

HEAD_DIM = 128
BLOCK = 128
PAGE = 8


def rows_first(arrays, axis, dims):
    turned = [jnp.moveaxis(a, dim, 0) for a, dim in zip(arrays, dims)]
    widths = [t[0].size for t in turned]
    both = jnp.concatenate([t.reshape(-1, w) for t, w in zip(turned, widths)], axis=1)
    result = lax.all_gather(both, axis, axis=0, tiled=True)
    tiles = jnp.split(result, [sum(widths[:k]) for k in range(1, len(widths))], axis=1)
    return tuple(
        (
            jnp.moveaxis(b.reshape(-1, *t.shape[1:]), 0, dim)
            for b, t, dim in zip(tiles, turned, dims)
        )
    )


def in_one_piece(arrays, axis, dim, along):
    columns = [a.reshape(*a.shape[:along], -1) for a in arrays]
    both = jnp.concatenate(columns, axis=along)
    result, at, gathered = (lax.all_gather(both, axis, axis=dim, tiled=True), 0, [])
    for a, column in zip(arrays, columns):
        section = result[..., at : at + column.shape[along]]
        gathered.append(section.reshape(*section.shape[:along], *a.shape[along:]))
        at += column.shape[along]
    return tuple(gathered)


def rotate(values, positions):
    half_dim = values.shape[-1] // 2
    freq_index = jnp.arange(half_dim, dtype=jnp.float32)
    inverse = jnp.exp(freq_index * (-2.0 * math.log(1000000.0) / values.shape[-1]))
    angles = positions.astype(jnp.float32)[..., None, None] * inverse
    cosine = jnp.cos(angles)
    sine = jnp.sin(angles)
    first_half = values[..., :half_dim]
    second_half = values[..., half_dim:]
    return jnp.concatenate(
        [first_half * cosine - second_half * sine, second_half * cosine + first_half * sine],
        axis=-1,
    )


def attend(query, key_new, value_new, key_old, value_old, prefix_mine, suffix_mine):
    batch, block_len, heads_here, head_dim = query.shape
    kv_here = key_new.shape[2]
    group_size = heads_here // kv_here
    old_len = key_old.shape[1]
    grouped = query.reshape(batch, block_len, kv_here, group_size, head_dim)
    all_keys = jnp.concatenate([key_old, key_new], axis=1)
    all_values = jnp.concatenate([value_old, value_new], axis=1)
    scores = jnp.einsum(
        "btkgd,bskd->bkgts", grouped, all_keys, preferred_element_type=jnp.float32
    ) / math.sqrt(head_dim)
    key_pos = jnp.arange(old_len + block_len, dtype=jnp.int32)
    query_pos = jnp.arange(block_len, dtype=jnp.int32)
    in_prefix = key_pos[None, None, :] < prefix_mine[:, None, None]
    shifted = key_pos - old_len
    in_suffix = (shifted[None, None, :] <= query_pos[None, :, None]) & (
        shifted[None, None, :] < suffix_mine[:, None, None]
    )
    allowed = jnp.where(key_pos[None, None, :] < old_len, in_prefix, in_suffix)[:, None, None]
    masked = jnp.where(allowed, scores, -1e30)
    peak = jnp.max(masked, axis=-1, keepdims=True)
    weights = jnp.where(allowed, jnp.exp(masked - peak), 0.0)
    probs = (weights / jnp.sum(weights, axis=-1, keepdims=True)).astype(jnp.bfloat16)
    mixed = jnp.einsum("bkgts,bskd->btkgd", probs, all_values, preferred_element_type=jnp.float32)
    live = query_pos[None, :] < suffix_mine[:, None]
    mixed = jnp.where(live[:, :, None, None, None], mixed, 0.0)
    return mixed.reshape(batch * block_len, heads_here * head_dim).astype(jnp.bfloat16)


def body(
    tokens,
    norm_gain,
    w_query,
    w_kv,
    b_query,
    b_kv,
    kv_pool,
    prefix_pages,
    prefix_len,
    suffix_len,
    fresh_owner,
):
    seq_count = lax.axis_size("seq")
    my_group = lax.axis_index("seq")
    token_rows = tokens.shape[0]
    blocks_here = token_rows // BLOCK
    kv_width = w_kv.shape[2]
    kv_here = kv_width // HEAD_DIM
    query_width = w_query.shape[1]
    heads_here = query_width // HEAD_DIM
    pool_pages = kv_pool.shape[0]
    page_slots = prefix_pages.shape[1]
    prefix_entries = blocks_here * page_slots
    suffix_pages = BLOCK // PAGE
    fresh_entries = blocks_here * suffix_pages
    prefix_cap = max(3, prefix_entries // seq_count + 1)
    fresh_cap = max(2, (fresh_entries + seq_count - 1) // seq_count + 1)
    first_row = my_group * blocks_here
    prefix_mine = lax.dynamic_slice_in_dim(prefix_len, first_row, blocks_here)
    suffix_mine = lax.dynamic_slice_in_dim(suffix_len, first_row, blocks_here)
    owners_mine = lax.dynamic_slice_in_dim(
        fresh_owner[:, 0], first_row * suffix_pages, fresh_entries
    )
    gathered, gain_whole = rows_first((tokens, norm_gain), "tp", (1, 0))
    widened = gathered.astype(jnp.float32)
    mean_square = jnp.mean(widened * widened, axis=-1, keepdims=True)
    normed = (widened * lax.rsqrt(mean_square + 1e-06) * gain_whole.astype(jnp.float32)).astype(
        jnp.bfloat16
    )
    all_ids = prefix_pages.reshape(seq_count, prefix_entries)
    all_owner = all_ids // pool_pages
    entry_ids = jnp.arange(prefix_entries, dtype=jnp.int32)
    before = (all_owner[:, :, None] == all_owner[:, None, :]) & (
        entry_ids[None, None, :] < entry_ids[None, :, None]
    )
    all_rank = jnp.sum(before.astype(jnp.int32), axis=-1)
    prefix_slots = jnp.arange(prefix_cap, dtype=jnp.int32)
    chosen = (all_owner[:, None, :] == my_group) & (
        all_rank[:, None, :] == prefix_slots[None, :, None]
    )
    picked = jnp.sum(jnp.where(chosen, entry_ids[None, None, :], 0), axis=-1)
    local_page = jnp.take_along_axis(all_ids, picked, axis=1) % pool_pages
    prefix_send = kv_pool[local_page]
    prefix_got = lax.all_to_all(prefix_send, "seq", split_axis=0, concat_axis=0, tiled=True)
    pieces = in_one_piece((w_query, w_kv), "seq", 0, 1)
    query_sums, pair_sums = tuple(
        (
            jnp.dot(
                normed,
                weight_piece.reshape(weight_piece.shape[0], -1),
                preferred_element_type=jnp.float32,
            )
            for weight_piece in pieces
        )
    )
    pair_lin = pair_sums + b_kv.reshape(1, 2 * kv_width)
    slot_ids = jnp.arange(BLOCK, dtype=jnp.int32)
    positions = prefix_mine[:, None] + slot_ids[None, :]
    live = (slot_ids[None, :] < suffix_mine[:, None])[:, :, None, None]
    key_new = jnp.where(
        live,
        rotate(pair_lin[:, :kv_width].reshape(blocks_here, BLOCK, kv_here, HEAD_DIM), positions),
        0.0,
    ).astype(jnp.bfloat16)
    value_new = jnp.where(
        live, pair_lin[:, kv_width:].reshape(blocks_here, BLOCK, kv_here, HEAD_DIM), 0.0
    ).astype(jnp.bfloat16)
    new_pages = jnp.stack(
        [
            key_new.reshape(fresh_entries, PAGE, kv_width),
            value_new.reshape(fresh_entries, PAGE, kv_width),
        ],
        axis=1,
    )
    fresh_ids = jnp.arange(fresh_entries, dtype=jnp.int32)
    fresh_before = (owners_mine[None, :] == owners_mine[:, None]) & (
        fresh_ids[None, :] < fresh_ids[:, None]
    )
    fresh_rank = jnp.sum(fresh_before.astype(jnp.int32), axis=1)
    group_ids = jnp.arange(seq_count, dtype=jnp.int32)
    fresh_slots = jnp.arange(fresh_cap, dtype=jnp.int32)
    placed = (owners_mine[None, None, :] == group_ids[:, None, None]) & (
        fresh_rank[None, None, :] == fresh_slots[None, :, None]
    )
    source = jnp.sum(jnp.where(placed, fresh_ids[None, None, :], 0), axis=-1)
    filled = jnp.any(placed, axis=-1)
    fresh_send = jnp.where(
        filled[:, :, None, None, None], new_pages[source], jnp.zeros((), jnp.bfloat16)
    )
    fresh_got = lax.all_to_all(fresh_send, "seq", split_axis=0, concat_axis=0, tiled=True)
    query_lin = query_sums + b_query[None, :]
    query = rotate(query_lin.reshape(blocks_here, BLOCK, heads_here, HEAD_DIM), positions).astype(
        jnp.bfloat16
    )
    my_rank = lax.dynamic_index_in_dim(all_rank, my_group, 0, keepdims=False)
    my_ids = lax.dynamic_index_in_dim(all_ids, my_group, 0, keepdims=False)
    arrived_at = my_ids // pool_pages * prefix_cap + my_rank
    fetched = prefix_got.reshape(seq_count * prefix_cap, 2, PAGE, kv_width)[arrived_at]
    fetched = fetched.reshape(blocks_here, page_slots, 2, PAGE, kv_here, HEAD_DIM)
    key_old = fetched[:, :, 0].reshape(blocks_here, page_slots * PAGE, kv_here, HEAD_DIM)
    value_old = fetched[:, :, 1].reshape(blocks_here, page_slots * PAGE, kv_here, HEAD_DIM)
    attn_out = attend(query, key_new, value_new, key_old, value_old, prefix_mine, suffix_mine)
    fresh_out = fresh_got.reshape(seq_count * fresh_cap, 2, PAGE, kv_width)
    return (attn_out, fresh_out)


def solution(mesh):
    placed = (
        P(("parts", "seq"), "tp"),
        P("tp"),
        P("seq", "tp"),
        P("seq", None, "tp"),
        P("tp"),
        P(None, "tp"),
        P(("parts", "seq"), None, None, "tp"),
        P("parts", None),
        P("parts"),
        P("parts"),
        P("parts", None),
    )
    return jax.shard_map(
        body,
        mesh=mesh,
        in_specs=placed,
        out_specs=(P(("parts", "seq"), "tp"), P(("parts", "seq"), None, None, "tp")),
        check_vma=False,
    )
```

profile of v0, /device:TPU:34, one launch (start us, length us, event | category | flops | bytes accessed | tf_op | source)
XLA Modules:
  0.0 323.7 jit_solution(4493974345548147127)
XLA Ops:
  7.2 0.1 all-gather.3.cloned.1.call-start
  7.3 0.7 reshape.693
  8.0 1.9 pad_maximum_fusion
  9.9 0.1 all-gather.3.cloned.1.call-update
  9.9 0.1 all-gather.5.cloned.1.call-start
  10.0 0.9 copy.65
  10.9 1.7 pad_maximum_fusion.1
  12.7 0.1 all-gather.5.cloned.1.call-update
  12.7 0.8 copy.35
  13.5 0.1 reshape.690
  13.6 0.9 convert_reduce_fusion
  14.6 0.1 select_reduce_fusion
  14.7 0.1 copy.36
  14.8 0.1 reshape.728
  15.0 1.3 gather_fusion.3
  16.3 0.1 gather.16
  16.4 0.1 copy.37
  16.5 0.1 copy.38
  16.6 0.1 reshape.706
  16.7 1.4 gather_fusion
  18.1 45.8 %all-to-all-start = ((bf16[32,3,2,8,128]{4,3,2,1,0:T(8,128)(2,1)}), bf16[32,3,2,8,128]{4,3,2,1,0:T(8,128)(2,1)S(1)}, u32[]{:S(2)}, u32[]{:S(2)}) async-start(bf16[32,3,2,8,128]{4,3,2,1,0:T(8,128)(2,1)} %bitcast.1), calls=%async_computation | async-start | bytes 786432 | tf_op jit(solution)/shard_map/all_to_all | solution.py:136
  63.9 0.7 fusion.46
  64.6 0.2 convert_reduce_fusion.1
  64.8 0.1 dynamic_slice.19
  64.9 0.1 dynamic_slice.16
  65.0 0.1 lt.238
  65.0 0.1 lt.239
  65.1 0.1 fusion.38
  65.3 0.1 copy.48
  65.3 0.1 reshape.722
  65.5 0.1 and_reduce_fusion
  65.6 0.1 copy.47
  65.7 0.1 bitcast_compare_fusion
  65.9 0.1 iota_compare_fusion.8
  65.9 0.1 add_convert_fusion.1
  66.0 0.1 iota_compare_fusion.5
  66.1 0.1 iota_compare_fusion
  66.2 0.3 and_select_fusion
  66.5 0.5 multiply_cosine_fusion
  67.1 50.0 %all-to-all-done = bf16[32,3,2,8,128]{4,3,2,1,0:T(8,128)(2,1)S(1)} async-done(((bf16[32,3,2,8,128]{4,3,2,1,0:T(8,128)(2,1)}), bf16[32,3,2,8,128]{4,3,2,1,0:T(8,128)(2,1)S(1)}, u32[]{:S(2)}, u32[]{:S(2)}) %all-to-all-start) | async-done | bytes 393248 | tf_op jit(solution)/shard_map/all_to_all | solution.py:136
  117.0 0.6 gather_fusion.1
  117.7 0.1 copy.40
  117.9 3.1 fusion
  121.0 0.9 slice_convert_fusion
  122.0 129.7 %all-gather.5.cloned.1.call-done = bf16[8192,768]{1,0:T(8,128)(2,1)} async-done(((bf16[256,768]{1,0:T(8,128)(2,1)}), bf16[8192,768]{1,0:T(8,128)(2,1)}) %all-gather.5.cloned.1.call-update) | async-done | bytes 12582928 | tf_op jit(solution)/shard_map/all_gather | solution.py:30
  251.7 4.8 %fusion.14 = f32[256,256]{1,0:T(8,128)S(1)} fusion(bf16[8192,768]{1,0:T(8,128)(2,1)} %all-gather.5.cloned.1.call-done, f32[8192]{0:T(1024)S(1)} %bitcast.112, f32[256]{0:T(256)S(1)} %add_rsqrt_fusion, bf16[8192,257]{0,1:T(8,128)(2,1)} %all-gather.3.cloned.1.call-done, f32[256]{0:T(256)S(1)} %bitcast.114), kind=kOutput, calls=%fused_computation.22 | convolution fusion | flops 1082195968 | bytes 8685568 | tf_op jit(solution)/shard_map/dot_general | solution.py:140
  256.5 0.6 fusion.32
  257.1 0.1 fusion.35
  257.2 0.7 gather_fusion.2
  257.9 0.8 broadcast_select_fusion
  258.7 16.0 %all-to-all-start.1 = ((bf16[32,2,2,8,128]{4,3,2,1,0:T(8,128)(2,1)}), bf16[32,2,2,8,128]{4,3,2,1,0:T(8,128)(2,1)S(1)}, u32[]{:S(2)}, u32[]{:S(2)}) async-start(bf16[32,2,2,8,128]{4,3,2,1,0:T(8,128)(2,1)} %broadcast_select_fusion), calls=%async_computation.1 | async-start | bytes 524288 | tf_op jit(solution)/shard_map/all_to_all | solution.py:182
  274.8 7.0 %fusion.8 = f32[256,512]{1,0:T(8,128)S(1)} fusion(bf16[8192,768]{1,0:T(8,128)(2,1)} %all-gather.5.cloned.1.call-done, f32[8192]{0:T(1024)S(1)} %bitcast.113, f32[256]{0:T(256)S(1)} %add_rsqrt_fusion, bf16[8192,257]{0,1:T(8,128)(2,1)} %all-gather.3.cloned.1.call-done, f32[512]{0:T(512)S(1)} %copy-done.1), kind=kOutput, calls=%fused_computation.18 | convolution fusion | flops 2156003328 | bytes 13143040 | tf_op jit(solution)/shard_map/dot_general | solution.py:140
  281.8 0.2 reshape.699
  282.0 0.1 select_convert_fusion
  282.1 0.1 copy.41
  282.3 0.3 fusion.51
  282.6 0.1 subtract_convert_fusion
  282.8 0.5 fusion.52
  283.2 0.3 fusion.7
  283.5 0.5 fusion.13
  284.1 0.2 copy.46
  284.3 0.7 copy.64
  285.0 31.1 %all-to-all-done.1 = bf16[32,2,2,8,128]{4,3,2,1,0:T(8,128)(2,1)S(1)} async-done(((bf16[32,2,2,8,128]{4,3,2,1,0:T(8,128)(2,1)}), bf16[32,2,2,8,128]{4,3,2,1,0:T(8,128)(2,1)S(1)}, u32[]{:S(2)}, u32[]{:S(2)}) %all-to-all-start.1) | async-done | bytes 262176 | tf_op jit(solution)/shard_map/all_to_all | solution.py:182
  316.1 0.7 copy.67
  (31 shorter events, 0.3 us)
Async XLA Ops:
  7.2 9.5 %copy-start = (bf16[128,2,8,128]{3,2,1,0:T(8,128)(2,1)S(1)}, bf16[128,2,8,128]{3,2,1,0:T(8,128)(2,1)}, u32[]{:S(2)}) copy-start(bf16[128,2,8,128]{3,2,1,0:T(8,128)(2,1)} %param.17) | copy-start | bytes 1572868
  7.2 110.7 %all-gather.3.cloned.1.call-start = ((), (), s32[]{:S(2)}) async-start(), calls=%async_computation.2 | async-start | bytes 4866048 | tf_op jit(solution)/shard_map/all_gather | solution.py:17
  9.9 241.7 %all-gather.5.cloned.1.call-start = ((), (), s32[]{:S(2)}) async-start(), calls=%async_computation.3 | async-start | bytes 12976128 | tf_op jit(solution)/shard_map/all_gather | solution.py:30
  14.9 49.9 %copy-start.3 = (s32[64]{0:T(128)S(1)}, s32[64]{0:T(128)}, u32[]{:S(2)}) copy-start(s32[64]{0:T(128)} %param.19) | copy-start | bytes 772
  15.0 49.9 %copy-start.4 = (s32[64]{0:T(128)S(1)}, s32[64]{0:T(128)}, u32[]{:S(2)}) copy-start(s32[64]{0:T(128)} %param.20) | copy-start | bytes 772
  16.2 235.4 %copy-start.2 = (f32[2,128]{1,0:T(2,128)S(1)}, f32[2,128]{1,0:T(2,128)}, u32[]{:S(2)}) copy-start(f32[2,128]{1,0:T(2,128)} %param.16) | copy-start | bytes 3076
  18.1 98.9 %all-to-all-start = ((bf16[32,3,2,8,128]{4,3,2,1,0:T(8,128)(2,1)}), bf16[32,3,2,8,128]{4,3,2,1,0:T(8,128)(2,1)S(1)}, u32[]{:S(2)}, u32[]{:S(2)}) async-start(bf16[32,3,2,8,128]{4,3,2,1,0:T(8,128)(2,1)} %bitcast.1), calls=%async_computation | async-start | bytes 786432 | tf_op jit(solution)/shard_map/all_to_all | solution.py:136
  251.7 23.1 %copy-start.1 = (f32[512]{0:T(512)S(1)}, f32[512]{0:T(512)}, u32[]{:S(2)}) copy-start(f32[512]{0:T(512)} %param.15) | copy-start | bytes 6148
  258.7 57.4 %all-to-all-start.1 = ((bf16[32,2,2,8,128]{4,3,2,1,0:T(8,128)(2,1)}), bf16[32,2,2,8,128]{4,3,2,1,0:T(8,128)(2,1)S(1)}, u32[]{:S(2)}, u32[]{:S(2)}) async-start(bf16[32,2,2,8,128]{4,3,2,1,0:T(8,128)(2,1)} %broadcast_select_fusion), calls=%async_computation.1 | async-start | bytes 524288 | tf_op jit(solution)/shard_map/all_to_all | solution.py:182
Sparse Core Ops, SparseCore 0:
  10.2 72.3 all-gather.2
  84.7 166.9 all-gather.4
where the time goes:
time: 324 us
  waiting for transfers between devices  211 us (65%)
  starting transfers between devices  61.9 us (19%)
  between operations  14.4 us (4%)
  matrix products  12.8 us (4%)
  other arithmetic  12.7 us (4%)
  local copies, waits for them, and re-layouts  10.9 us (3%)
    all_gather x1, waiting for transfers between devices, in_one_piece(): lax.all_gather(both, axis, axis=dim, tiled=True)  130 us
    all_to_all x1, waiting for transfers between devices, body(): lax.all_to_all(prefix_send, 'seq', split_axis=0, concat_axis=0, tiled=True)  50 us
    all_to_all x1, starting transfers between devices, body(): lax.all_to_all(prefix_send, 'seq', split_axis=0, concat_axis=0, tiled=True)  45.8 us
    all_to_all x1, waiting for transfers between devices, body(): lax.all_to_all(fresh_send, 'seq', split_axis=0, concat_axis=0, tiled=True)  31.1 us
    all_to_all x1, starting transfers between devices, body(): lax.all_to_all(fresh_send, 'seq', split_axis=0, concat_axis=0, tiled=True)  16 us
    dot_general x2, matrix products, body(): jnp.dot(normed, weight_piece.reshape(weight_piece.shape[0], -1), preferre...  11.8 us
  transfers between devices with their start and end apart: 4, of which 3 were waited for; matrix products, arithmetic and copies ran while one was open for 8% of the time, Pallas kernels for 0%

commit v1 on v0

--- a/solution.py
+++ b/solution.py
@@ -8,31 +8,7 @@
 HEAD_DIM = 128
 BLOCK = 128
 PAGE = 8
-
-
-def rows_first(arrays, axis, dims):
-    turned = [jnp.moveaxis(a, dim, 0) for a, dim in zip(arrays, dims)]
-    widths = [t[0].size for t in turned]
-    both = jnp.concatenate([t.reshape(-1, w) for t, w in zip(turned, widths)], axis=1)
-    result = lax.all_gather(both, axis, axis=0, tiled=True)
-    tiles = jnp.split(result, [sum(widths[:k]) for k in range(1, len(widths))], axis=1)
-    return tuple(
-        (
-            jnp.moveaxis(b.reshape(-1, *t.shape[1:]), 0, dim)
-            for b, t, dim in zip(tiles, turned, dims)
-        )
-    )
-
-
-def in_one_piece(arrays, axis, dim, along):
-    columns = [a.reshape(*a.shape[:along], -1) for a in arrays]
-    both = jnp.concatenate(columns, axis=along)
-    result, at, gathered = (lax.all_gather(both, axis, axis=dim, tiled=True), 0, [])
-    for a, column in zip(arrays, columns):
-        section = result[..., at : at + column.shape[along]]
-        gathered.append(section.reshape(*section.shape[:along], *a.shape[along:]))
-        at += column.shape[along]
-    return tuple(gathered)
+CORES = 2
 
 
 def rotate(values, positions):
@@ -79,6 +55,43 @@
     return mixed.reshape(batch * block_len, heads_here * head_dim).astype(jnp.bfloat16)
 
 
+def swap_parts(value):
+    count = lax.axis_size("parts")
+    return lax.ppermute(value, "parts", [(i, i ^ 1) for i in range(count)])
+
+
+def swap_cores(value):
+    count = lax.axis_size("tp")
+    return lax.ppermute(value, "tp", [(i, i ^ 1) for i in range(count)])
+
+
+def shift_chips(value, by):
+    count = lax.axis_size("tp")
+    return lax.ppermute(value, "tp", [(i, (i + by * CORES) % count) for i in range(count)])
+
+
+def gather_chips(own):
+    half = own.shape[0] // 2
+    from_left = shift_chips(own, 1)
+    from_right = shift_chips(own, -1)
+    own_other = swap_cores(own)
+    far_top = shift_chips(from_left[:half], 1)
+    far_low = shift_chips(from_right[half:], -1)
+    left_other = swap_cores(from_left)
+    right_other = swap_cores(from_right)
+    far = jnp.concatenate([far_top, far_low], axis=0)
+    far_other = swap_cores(far)
+    return [
+        (own, own_other),
+        (from_left, left_other),
+        (from_right, right_other),
+        (far, far_other),
+    ]
+
+
+STEPS = (0, -1, 1, 2)
+
+
 def body(
     tokens,
     norm_gain,
@@ -93,13 +106,18 @@
     fresh_owner,
 ):
     seq_count = lax.axis_size("seq")
+    tp_count = lax.axis_size("tp")
     my_group = lax.axis_index("seq")
-    token_rows = tokens.shape[0]
+    my_tp = lax.axis_index("tp")
+    parity = lax.axis_index("parts") % 2
+    token_rows, feat = tokens.shape
     blocks_here = token_rows // BLOCK
     kv_width = w_kv.shape[2]
     kv_here = kv_width // HEAD_DIM
     query_width = w_query.shape[1]
+    half_width = query_width // 2
     heads_here = query_width // HEAD_DIM
+    half_heads = heads_here // 2
     pool_pages = kv_pool.shape[0]
     page_slots = prefix_pages.shape[1]
     prefix_entries = blocks_here * page_slots
@@ -113,12 +131,37 @@
     owners_mine = lax.dynamic_slice_in_dim(
         fresh_owner[:, 0], first_row * suffix_pages, fresh_entries
     )
-    gathered, gain_whole = rows_first((tokens, norm_gain), "tp", (1, 0))
-    widened = gathered.astype(jnp.float32)
-    mean_square = jnp.mean(widened * widened, axis=-1, keepdims=True)
-    normed = (widened * lax.rsqrt(mean_square + 1e-06) * gain_whole.astype(jnp.float32)).astype(
-        jnp.bfloat16
-    )
+
+    w_pair_half = lax.dynamic_index_in_dim(w_kv, parity, 1, keepdims=False)
+    w_query_half = lax.dynamic_slice_in_dim(w_query, parity * half_width, half_width, axis=1)
+    w_pair_all = lax.all_gather(w_pair_half, "seq", axis=0, tiled=True)
+    w_query_all = lax.all_gather(w_query_half, "seq", axis=0, tiled=True)
+    b_pair_half = lax.dynamic_index_in_dim(b_kv, parity, 0, keepdims=True)
+    b_query_half = lax.dynamic_slice_in_dim(b_query, parity * half_width, half_width)[None]
+
+    gain_rows = jnp.broadcast_to(norm_gain[None], (16, feat))
+    mine_ext = jnp.concatenate([gain_rows, tokens], axis=0)
+    other_tokens = swap_parts(tokens)
+    other_prefix = swap_parts(prefix_mine)
+    pieces_mine = gather_chips(mine_ext)
+    pieces_other = gather_chips(other_tokens)
+
+    square = jnp.zeros((2 * token_rows, 1), jnp.float32)
+    raw = []
+    for mine, other, step in zip(pieces_mine, pieces_other, STEPS):
+        for core in range(CORES):
+            rows = jnp.concatenate([mine[core][16:], other[core]], axis=0)
+            gain = mine[core][:1]
+            at = ((my_tp + step * CORES) % tp_count) ^ core
+            wide = rows.astype(jnp.float32)
+            square = square + jnp.sum(wide * wide, axis=-1, keepdims=True)
+            raw.append((rows, gain, at))
+    scale = lax.rsqrt(square / (feat * tp_count) + 1e-06)
+    normed = jnp.zeros((2 * token_rows, feat * tp_count), jnp.bfloat16)
+    for rows, gain, at in raw:
+        done = (rows.astype(jnp.float32) * scale * gain.astype(jnp.float32)).astype(jnp.bfloat16)
+        normed = lax.dynamic_update_slice_in_dim(normed, done, at * feat, axis=1)
+
     all_ids = prefix_pages.reshape(seq_count, prefix_entries)
     all_owner = all_ids // pool_pages
     entry_ids = jnp.arange(prefix_entries, dtype=jnp.int32)
@@ -134,29 +177,20 @@
     local_page = jnp.take_along_axis(all_ids, picked, axis=1) % pool_pages
     prefix_send = kv_pool[local_page]
     prefix_got = lax.all_to_all(prefix_send, "seq", split_axis=0, concat_axis=0, tiled=True)
-    pieces = in_one_piece((w_query, w_kv), "seq", 0, 1)
-    query_sums, pair_sums = tuple(
-        (
-            jnp.dot(
-                normed,
-                weight_piece.reshape(weight_piece.shape[0], -1),
-                preferred_element_type=jnp.float32,
-            )
-            for weight_piece in pieces
-        )
-    )
-    pair_lin = pair_sums + b_kv.reshape(1, 2 * kv_width)
+
     slot_ids = jnp.arange(BLOCK, dtype=jnp.int32)
-    positions = prefix_mine[:, None] + slot_ids[None, :]
+    both_prefix = jnp.concatenate([prefix_mine, other_prefix])
+    positions = both_prefix[:, None] + slot_ids[None, :]
     live = (slot_ids[None, :] < suffix_mine[:, None])[:, :, None, None]
-    key_new = jnp.where(
-        live,
-        rotate(pair_lin[:, :kv_width].reshape(blocks_here, BLOCK, kv_here, HEAD_DIM), positions),
-        0.0,
-    ).astype(jnp.bfloat16)
-    value_new = jnp.where(
-        live, pair_lin[:, kv_width:].reshape(blocks_here, BLOCK, kv_here, HEAD_DIM), 0.0
-    ).astype(jnp.bfloat16)
+    pair_lin = jnp.dot(normed, w_pair_all, preferred_element_type=jnp.float32) + b_pair_half
+    pair_lin = pair_lin.reshape(2 * blocks_here, BLOCK, kv_here, HEAD_DIM)
+    pair_half = jnp.where(parity == 0, rotate(pair_lin, positions), pair_lin).astype(jnp.bfloat16)
+    pair_kept = pair_half[:blocks_here]
+    pair_got = swap_parts(pair_half[blocks_here:])
+    zero = jnp.zeros((), jnp.bfloat16)
+    key_new = jnp.where(live, jnp.where(parity == 0, pair_kept, pair_got), zero)
+    value_new = jnp.where(live, jnp.where(parity == 0, pair_got, pair_kept), zero)
+
     new_pages = jnp.stack(
         [
             key_new.reshape(fresh_entries, PAGE, kv_width),
@@ -176,14 +210,23 @@
     )
     source = jnp.sum(jnp.where(placed, fresh_ids[None, None, :], 0), axis=-1)
     filled = jnp.any(placed, axis=-1)
-    fresh_send = jnp.where(
-        filled[:, :, None, None, None], new_pages[source], jnp.zeros((), jnp.bfloat16)
-    )
+    fresh_send = jnp.where(filled[:, :, None, None, None], new_pages[source], zero)
     fresh_got = lax.all_to_all(fresh_send, "seq", split_axis=0, concat_axis=0, tiled=True)
-    query_lin = query_sums + b_query[None, :]
-    query = rotate(query_lin.reshape(blocks_here, BLOCK, heads_here, HEAD_DIM), positions).astype(
-        jnp.bfloat16
-    )
+
+    query_lin = jnp.dot(normed, w_query_all, preferred_element_type=jnp.float32) + b_query_half
+    query_half = rotate(
+        query_lin.reshape(2 * blocks_here, BLOCK, half_heads, HEAD_DIM), positions
+    ).astype(jnp.bfloat16)
+    query_kept = query_half[:blocks_here]
+    query_got = swap_parts(query_half[blocks_here:])
+    query = jnp.concatenate(
+        [
+            jnp.where(parity == 0, query_kept, query_got),
+            jnp.where(parity == 0, query_got, query_kept),
+        ],
+        axis=2,
+    )
+
     my_rank = lax.dynamic_index_in_dim(all_rank, my_group, 0, keepdims=False)
     my_ids = lax.dynamic_index_in_dim(all_ids, my_group, 0, keepdims=False)
     arrived_at = my_ids // pool_pages * prefix_cap + my_rank

time: 324 us -> 361 us (1.11)
  starting transfers between devices: 61.9 us -> 113 us
  waiting for transfers between devices: 211 us -> 176 us
  other arithmetic: 12.7 us -> 21.8 us
  local copies, waits for them, and re-layouts: 10.9 us -> 19 us
    ppermute x0 -> x20, starting transfers between devices: none -> 91.3 us  [the longest x8 60.7 us: shift_chips(): lax.ppermute(value, 'tp', [(i, (i + by * CORES) % count) for i in range(c...]
    all_to_all x1, waiting for transfers between devices: 50 us -> 0.01 us  [body(): lax.all_to_all(prefix_send, 'seq', split_axis=0, concat_axis=0, tiled=True)]
    all_to_all x1, starting transfers between devices: 45.8 us -> 7.48 us  [body(): lax.all_to_all(prefix_send, 'seq', split_axis=0, concat_axis=0, tiled=True)]
    all_to_all x1, waiting for transfers between devices: 31.1 us -> 0.01 us  [body(): lax.all_to_all(fresh_send, 'seq', split_axis=0, concat_axis=0, tiled=True)]
    all_gather x2, waiting for transfers between devices: 130 us -> 159 us  [the longest x1 113 us: body(): w_query_all = lax.all_gather(w_query_half, 'seq', axis=0, tiled=True)]
    ppermute x0 -> x20, waiting for transfers between devices: none -> 17.2 us  [the longest x8 10.1 us: shift_chips(): lax.ppermute(value, 'tp', [(i, (i + by * CORES) % count) for i in range(c...]
    dynamic_update_slice x0 -> x8, other arithmetic: none -> 10.5 us  [body(): normed = lax.dynamic_update_slice_in_dim(normed, done, at * feat, axis=1)]
    broadcast_in_dim x0 -> x2, local copies, waits for them, and re-layouts: none -> 4.93 us  [the longest x1 4.24 us: body(): normed = jnp.zeros((2 * token_rows, feat * tp_count), jnp.bfloat16)]
  transfers between devices with their start and end apart: 4 -> 24, of which waited for: 3 -> 9; matrix products, arithmetic and copies ran while one was open for 8% -> 14% of each run, Pallas kernels for 0% -> 0%
where the time goes in v1:
time: 361 us; the launch traced here: 359 us
  waiting for transfers between devices  176 us (49%)
  starting transfers between devices  113 us (31%)
  other arithmetic  21.8 us (6%)
  local copies, waits for them, and re-layouts  19 us (5%)
  between operations  15 us (4%)
  matrix products  14.2 us (4%)
    all_gather x1, waiting for transfers between devices, body(): w_query_all = lax.all_gather(w_query_half, 'seq', axis=0, tiled=True)  113 us
    ppermute x8, starting transfers between devices, shift_chips(): lax.ppermute(value, 'tp', [(i, (i + by * CORES) % count) for i in range(c...  60.7 us
    all_gather x1, waiting for transfers between devices, body(): w_pair_all = lax.all_gather(w_pair_half, 'seq', axis=0, tiled=True)  46.2 us
    ppermute x8, starting transfers between devices, swap_cores(): return lax.ppermute(value, 'tp', [(i, i ^ 1) for i in range(count)])  16.2 us
    ppermute x4, starting transfers between devices, swap_parts(): return lax.ppermute(value, 'parts', [(i, i ^ 1) for i in range(count)])  14.4 us
    all_to_all x1, starting transfers between devices, body(): lax.all_to_all(fresh_send, 'seq', split_axis=0, concat_axis=0, tiled=True)  14.3 us
    dynamic_update_slice x8, other arithmetic, body(): normed = lax.dynamic_update_slice_in_dim(normed, done, at * feat, axis=1)  10.5 us
    ppermute x8, waiting for transfers between devices, shift_chips(): lax.ppermute(value, 'tp', [(i, (i + by * CORES) % count) for i in range(c...  10.1 us
  transfers between devices with their start and end apart: 24, of which 9 were waited for; matrix products, arithmetic and copies ran while one was open for 14% of the time, Pallas kernels for 0%

profile of v1, /device:TPU:34, one launch (start us, length us, event | category | flops | bytes accessed | tf_op | source)
XLA Modules:
  0.0 359.5 jit_solution(15236164558337736232)
XLA Ops:
  7.3 1.1 constant_dynamic-slice_fusion.3
  8.4 0.6 copy.55
  9.1 4.1 %collective-permute-start = (bf16[256,1024]{1,0:T(8,128)(2,1)}, bf16[256,1024]{1,0:T(8,128)(2,1)S(1)}, u32[]{:S(2)}, u32[]{:S(2)}) collective-permute-start(bf16[256,1024]{1,0:T(8,128)(2,1)} %param.11), channel_id=1, source_target_pairs={{0,256},{256,0},{1,257},{257,1},{2,258},{258,2},{3,259},{259,3},{4... | collective-permute-start | bytes 1572872 | tf_op jit(solution)/shard_map/ppermute | solution.py:60
  13.2 0.7 broadcast_in_dim.108
  13.8 1.9 pad_maximum_fusion.8
  15.7 3.6 collective-permute-start.3
  19.3 38.6 %collective-permute-start.7 = (bf16[272,1024]{1,0:T(8,128)(2,1)}, bf16[272,1024]{1,0:T(8,128)(2,1)S(1)}, u32[]{:S(2)}, u32[]{:S(2)}) collective-permute-start(bf16[272,1024]{1,0:T(8,128)(2,1)} %pad_maximum_fusion.8), channel_id=1, source_target_pairs={{0,6},{1,7},{2,0},{3,1},{4,2},{5,3},{6,4},{7,5},{8,14},{9,15},{10,... | collective-permute-start | bytes 1671176 | tf_op jit(solution)/shard_map/ppermute | solution.py:70
  57.9 2.0 collective-permute-start.1
  59.9 0.7 dynamic_slice.35
  60.6 3.9 %collective-permute-start.17 = (s32[2]{0:T(128)S(1)}, s32[2]{0:T(128)S(1)}, u32[]{:S(2)}, u32[]{:S(2)}) collective-permute-start(s32[2]{0:T(128)S(1)} %dynamic_slice.35), channel_id=1, source_target_pairs={{0,256},{256,0},{1,257},{257,1},{2,258},{258,2},{3,259},{259,3},{4... | collective-permute-start | bytes 32 | tf_op jit(solution)/shard_map/ppermute | solution.py:60
  64.6 0.7 fusion.69
  65.8 0.8 copy.36
  66.7 0.9 convert_reduce_fusion
  68.1 1.3 gather_fusion.3
  69.8 1.4 gather_fusion
  71.2 7.5 %all-to-all-start = ((bf16[32,3,2,8,128]{4,3,2,1,0:T(8,128)(2,1)}), bf16[32,3,2,8,128]{4,3,2,1,0:T(8,128)(2,1)S(1)}, u32[]{:S(2)}, u32[]{:S(2)}) async-start(bf16[32,3,2,8,128]{4,3,2,1,0:T(8,128)(2,1)} %bitcast.1), calls=%async_computation | async-start | bytes 786432 | tf_op jit(solution)/shard_map/all_to_all | solution.py:179
  78.8 0.7 constant_dynamic-slice_fusion.1
  80.9 3.6 collective-permute-start.4
  84.5 2.3 collective-permute-start.8
  87.1 2.0 collective-permute-start.2
  89.1 3.6 collective-permute-start.11
  92.7 3.1 collective-permute-start.12
  95.9 0.7 slice_convert_fusion.6
  96.7 1.1 slice.122
  97.8 5.0 %collective-permute-done.11 = bf16[136,1024]{1,0:T(8,128)(2,1)S(1)} collective-permute-done((bf16[136,1024]{1,0:T(8,128)(2,1)S(1)}, bf16[136,1024]{1,0:T(8,128)(2,1)S(1)}, u32[]{:S(2)}, u32[]{:S(2)}) %collective-permute-start.11) | collective-permute-done | bytes 278560 | tf_op jit(solution)/shard_map/ppermute | solution.py:70
  102.8 1.9 collective-permute-start.5
  104.8 1.3 collective-permute-done.12
  106.1 1.9 collective-permute-start.9
  108.1 2.4 collective-permute-start.15
  110.6 3.3 collective-permute-start.13
  114.5 2.6 collective-permute-start.14
  117.4 2.0 collective-permute-start.10
  119.4 1.7 collective-permute-done.13
  121.1 1.9 collective-permute-start.6
  123.0 2.1 collective-permute-done.14
  125.2 2.1 collective-permute-start.16
  128.3 0.7 collective-permute-done.16
  129.3 4.2 %broadcast_in_dim.107 = bf16[512,8192]{1,0:T(8,128)(2,1)} broadcast(bf16[]{:T(256)} %constant.156.clone.1), dimensions={} | broadcast | bytes 8388610 | tf_op jit(solution)/shard_map/broadcast_in_dim | solution.py:160
  133.5 1.3 fusion.40
  134.8 1.3 fusion.39
  136.1 1.3 fusion.38
  137.5 1.3 fusion.37
  138.8 1.3 fusion.36
  140.1 1.4 fusion.35
  141.5 1.3 fusion.34
  142.8 1.3 fusion.33
  144.1 46.2 %all-gather.6.cloned.1.call-done = bf16[8192,1,128]{2,0,1:T(8,128)(2,1)} async-done(((bf16[256,1,128]{2,0,1:T(8,128)(2,1)}), bf16[8192,1,128]{2,0,1:T(8,128)(2,1)}) %all-gather.6.cloned.1.call-update) | async-done | bytes 2097168 | tf_op jit(solution)/shard_map/all_gather | solution.py:137
  190.3 6.4 %fusion.30 = f32[512,128]{1,0:T(8,128)S(1)} fusion(bf16[512,8192]{1,0:T(8,128)(2,1)} %fusion.33, bf16[8192,1,128]{2,0,1:T(8,128)(2,1)} %all-gather.6.cloned.1.call-done, f32[128]{0:T(128)S(1)} %fusion.68), kind=kOutput, calls=%fused_computation.55 | convolution fusion | flops 1073807360 | bytes 10748416 | tf_op jit(solution)/shard_map/dot_general | solution.py:185
  196.8 1.2 fusion.47
  198.1 3.4 collective-permute-start.18
  201.5 2.8 collective-permute-done.18
  204.4 0.7 gather_fusion.2
  205.1 0.8 broadcast_select_fusion
  205.9 14.3 %all-to-all-start.1 = ((bf16[32,2,2,8,128]{4,3,2,1,0:T(8,128)(2,1)}), bf16[32,2,2,8,128]{4,3,2,1,0:T(8,128)(2,1)S(1)}, u32[]{:S(2)}, u32[]{:S(2)}) async-start(bf16[32,2,2,8,128]{4,3,2,1,0:T(8,128)(2,1)} %broadcast_select_fusion), calls=%async_computation.1 | async-start | bytes 524288 | tf_op jit(solution)/shard_map/all_to_all | solution.py:214
  220.2 1.0 multiply_cosine_fusion
  221.2 0.6 gather_fusion.1
  221.8 112.8 %all-gather.4.cloned.1.call-done = bf16[8192,256]{1,0:T(8,128)(2,1)} async-done(((bf16[256,256]{1,0:T(8,128)(2,1)}), bf16[8192,256]{1,0:T(8,128)(2,1)}) %all-gather.4.cloned.1.call-update) | async-done | bytes 4194320 | tf_op jit(solution)/shard_map/all_gather | solution.py:138
  334.6 6.9 %convolution_add_fusion = f32[512,256]{1,0:T(8,128)S(1)} fusion(bf16[512,8192]{1,0:T(8,128)(2,1)} %fusion.33, bf16[8192,256]{1,0:T(8,128)(2,1)} %all-gather.4.cloned.1.call-done, f32[256]{0:T(256)S(1)} %dynamic_slice.37), kind=kOutput, calls=%fused_computation.51 | convolution fusion | flops 2147614720 | bytes 13108224 | tf_op jit(solution)/shard_map/dot_general | solution.py:216
  341.8 0.6 fusion.73
  342.7 3.0 collective-permute-start.19
  346.1 3.5 collective-permute-done.19
  350.5 0.5 fusion.29
  351.2 0.7 copy.65
  351.9 0.7 copy.76
  (112 shorter events, 7.6 us)
Async XLA Ops:
  7.2 62.6 %copy-start = (bf16[128,2,8,128]{3,2,1,0:T(8,128)(2,1)S(1)}, bf16[128,2,8,128]{3,2,1,0:T(8,128)(2,1)}, u32[]{:S(2)}) copy-start(bf16[128,2,8,128]{3,2,1,0:T(8,128)(2,1)} %param.17) | copy-start | bytes 1572868
  7.2 183.1 %all-gather.6.cloned.1.call-start = ((), (), s32[]{:S(2)}) async-start(), calls=%async_computation.3 | async-start | bytes 2162688 | tf_op jit(solution)/shard_map/all_gather | solution.py:137
  9.1 71.8 %collective-permute-start = (bf16[256,1024]{1,0:T(8,128)(2,1)}, bf16[256,1024]{1,0:T(8,128)(2,1)S(1)}, u32[]{:S(2)}, u32[]{:S(2)}) collective-permute-start(bf16[256,1024]{1,0:T(8,128)(2,1)} %param.11), channel_id=1, source_target_pairs={{0,256},{256,0},{1,257},{257,1},{2,258},{258,2},{3,259},{259,3},{4... | collective-permute-start | bytes 1572872 | tf_op jit(solution)/shard_map/ppermute | solution.py:60
  15.7 71.4 %collective-permute-start.3 = (bf16[272,1024]{1,0:T(8,128)(2,1)}, bf16[272,1024]{1,0:T(8,128)(2,1)S(1)}, u32[]{:S(2)}, u32[]{:S(2)}) collective-permute-start(bf16[272,1024]{1,0:T(8,128)(2,1)} %pad_maximum_fusion.8), channel_id=1, source_target_pairs={{0,2},{1,3},{2,4},{3,5},{4,6},{5,7},{6,0},{7,1},{8,10},{9,11},{10,... | collective-permute-start | bytes 1671176 | tf_op jit(solution)/shard_map/ppermute | solution.py:70
  19.3 69.8 %collective-permute-start.7 = (bf16[272,1024]{1,0:T(8,128)(2,1)}, bf16[272,1024]{1,0:T(8,128)(2,1)S(1)}, u32[]{:S(2)}, u32[]{:S(2)}) collective-permute-start(bf16[272,1024]{1,0:T(8,128)(2,1)} %pad_maximum_fusion.8), channel_id=1, source_target_pairs={{0,6},{1,7},{2,0},{3,1},{4,2},{5,3},{6,4},{7,5},{8,14},{9,15},{10,... | collective-permute-start | bytes 1671176 | tf_op jit(solution)/shard_map/ppermute | solution.py:70
  57.9 34.8 %collective-permute-start.1 = (bf16[272,1024]{1,0:T(8,128)(2,1)}, bf16[272,1024]{1,0:T(8,128)(2,1)}, u32[]{:S(2)}, u32[]{:S(2)}) collective-permute-start(bf16[272,1024]{1,0:T(8,128)(2,1)} %pad_maximum_fusion.8), channel_id=1, source_target_pairs={{0,1},{1,0},{2,3},{3,2},{4,5},{5,4},{6,7},{7,6},{8,9},{9,8},{10,11... | collective-permute-start | bytes 1671176 | tf_op jit(solution)/shard_map/ppermute | solution.py:65
  60.6 20.1 %collective-permute-start.17 = (s32[2]{0:T(128)S(1)}, s32[2]{0:T(128)S(1)}, u32[]{:S(2)}, u32[]{:S(2)}) collective-permute-start(s32[2]{0:T(128)S(1)} %dynamic_slice.35), channel_id=1, source_target_pairs={{0,256},{256,0},{1,257},{257,1},{2,258},{258,2},{3,259},{259,3},{4... | collective-permute-start | bytes 32 | tf_op jit(solution)/shard_map/ppermute | solution.py:60
  68.0 10.8 %copy-start.2 = (bf16[256,512]{1,0:T(8,128)(2,1)S(1)}, bf16[256,512]{1,0:T(8,128)(2,1)}, u32[]{:S(2)}) copy-start(bf16[256,512]{1,0:T(8,128)(2,1)} %param.13) | copy-start | bytes 786436
  68.0 11.5 %copy-start.6 = (s32[64]{0:T(128)S(1)}, s32[64]{0:T(128)}, u32[]{:S(2)}) copy-start(s32[64]{0:T(128)} %param.20) | copy-start | bytes 772
  69.3 11.1 %copy-start.5 = (f32[2,128]{1,0:T(2,128)S(1)}, f32[2,128]{1,0:T(2,128)}, u32[]{:S(2)}) copy-start(f32[2,128]{1,0:T(2,128)} %param.16) | copy-start | bytes 3076
  69.3 11.1 %copy-start.3 = (bf16[1024]{0:T(1024)(128)(2,1)S(1)}, bf16[1024]{0:T(1024)(128)(2,1)}, u32[]{:S(2)}) copy-start(bf16[1024]{0:T(1024)(128)(2,1)} %param.12) | copy-start | bytes 6148
  69.4 11.3 %copy-start.4 = (f32[512]{0:T(512)S(1)}, f32[512]{0:T(512)}, u32[]{:S(2)}) copy-start(f32[512]{0:T(512)} %param.15) | copy-start | bytes 6148
  69.4 17.4 %copy-start.1 = (bf16[256,1024]{1,0:T(8,128)(2,1)S(1)}, bf16[256,1024]{1,0:T(8,128)(2,1)}, u32[]{:S(2)}) copy-start(bf16[256,1024]{1,0:T(8,128)(2,1)} %param.11) | copy-start | bytes 1572868
  71.2 134.7 %all-to-all-start = ((bf16[32,3,2,8,128]{4,3,2,1,0:T(8,128)(2,1)}), bf16[32,3,2,8,128]{4,3,2,1,0:T(8,128)(2,1)S(1)}, u32[]{:S(2)}, u32[]{:S(2)}) async-start(bf16[32,3,2,8,128]{4,3,2,1,0:T(8,128)(2,1)} %bitcast.1), calls=%async_computation | async-start | bytes 786432 | tf_op jit(solution)/shard_map/all_to_all | solution.py:179
  78.7 255.9 %all-gather.4.cloned.1.call-start = ((), (), s32[]{:S(2)}) async-start(), calls=%async_computation.2 | async-start | bytes 4325376 | tf_op jit(solution)/shard_map/all_gather | solution.py:138
  80.9 27.2 %collective-permute-start.4 = (bf16[256,1024]{1,0:T(8,128)(2,1)S(1)}, bf16[256,1024]{1,0:T(8,128)(2,1)S(1)}, u32[]{:S(2)}, u32[]{:S(2)}) collective-permute-start(bf16[256,1024]{1,0:T(8,128)(2,1)S(1)} %collective-permute-done), channel_id=1, source_target_pairs={{0,2},{1,3},{2,4},{3,5},{4,6},{5,7},{6,0},{7,1},{8,10},{9,11},{10,... | collective-permute-start | bytes 1572872 | tf_op jit(solution)/shard_map/ppermute | solution.py:70
  84.5 26.2 %collective-permute-start.8 = (bf16[256,1024]{1,0:T(8,128)(2,1)S(1)}, bf16[256,1024]{1,0:T(8,128)(2,1)S(1)}, u32[]{:S(2)}, u32[]{:S(2)}) collective-permute-start(bf16[256,1024]{1,0:T(8,128)(2,1)S(1)} %collective-permute-done), channel_id=1, source_target_pairs={{0,6},{1,7},{2,0},{3,1},{4,2},{5,3},{6,4},{7,5},{8,14},{9,15},{10,... | collective-permute-start | bytes 1572872 | tf_op jit(solution)/shard_map/ppermute | solution.py:70
  87.1 27.4 %collective-permute-start.2 = (bf16[256,1024]{1,0:T(8,128)(2,1)S(1)}, bf16[256,1024]{1,0:T(8,128)(2,1)S(1)}, u32[]{:S(2)}, u32[]{:S(2)}) collective-permute-start(bf16[256,1024]{1,0:T(8,128)(2,1)S(1)} %collective-permute-done), channel_id=1, source_target_pairs={{0,1},{1,0},{2,3},{3,2},{4,5},{5,4},{6,7},{7,6},{8,9},{9,8},{10,11... | collective-permute-start | bytes 1572872 | tf_op jit(solution)/shard_map/ppermute | solution.py:65
  89.1 13.7 %collective-permute-start.11 = (bf16[136,1024]{1,0:T(8,128)(2,1)S(1)}, bf16[136,1024]{1,0:T(8,128)(2,1)S(1)}, u32[]{:S(2)}, u32[]{:S(2)}) collective-permute-start(bf16[136,1024]{1,0:T(8,128)(2,1)S(1)} %slice.127), channel_id=1, source_target_pairs={{0,2},{1,3},{2,4},{3,5},{4,6},{5,7},{6,0},{7,1},{8,10},{9,11},{10,... | collective-permute-start | bytes 835592 | tf_op jit(solution)/shard_map/ppermute | solution.py:70
  92.7 13.4 %collective-permute-start.12 = (bf16[136,1024]{1,0:T(8,128)(2,1)S(1)}, bf16[136,1024]{1,0:T(8,128)(2,1)S(1)}, u32[]{:S(2)}, u32[]{:S(2)}) collective-permute-start(bf16[136,1024]{1,0:T(8,128)(2,1)S(1)} %slice.128), channel_id=1, source_target_pairs={{0,6},{1,7},{2,0},{3,1},{4,2},{5,3},{6,4},{7,5},{8,14},{9,15},{10,... | collective-permute-start | bytes 835592 | tf_op jit(solution)/shard_map/ppermute | solution.py:70
  102.8 14.6 %collective-permute-start.5 = (bf16[272,1024]{1,0:T(8,128)(2,1)S(1)}, bf16[272,1024]{1,0:T(8,128)(2,1)S(1)}, u32[]{:S(2)}, u32[]{:S(2)}) collective-permute-start(bf16[272,1024]{1,0:T(8,128)(2,1)S(1)} %collective-permute-done.3), channel_id=1, source_target_pairs={{0,1},{1,0},{2,3},{3,2},{4,5},{5,4},{6,7},{7,6},{8,9},{9,8},{10,11... | collective-permute-start | bytes 1671176 | tf_op jit(solution)/shard_map/ppermute | solution.py:65
  106.1 21.2 %collective-permute-start.9 = (bf16[272,1024]{1,0:T(8,128)(2,1)S(1)}, bf16[272,1024]{1,0:T(8,128)(2,1)S(1)}, u32[]{:S(2)}, u32[]{:S(2)}) collective-permute-start(bf16[272,1024]{1,0:T(8,128)(2,1)S(1)} %collective-permute-done.7), channel_id=1, source_target_pairs={{0,1},{1,0},{2,3},{3,2},{4,5},{5,4},{6,7},{7,6},{8,9},{9,8},{10,11... | collective-permute-start | bytes 1671176 | tf_op jit(solution)/shard_map/ppermute | solution.py:65
  108.1 19.6 %collective-permute-start.15 = (bf16[272,1024]{1,0:T(8,128)(2,1)S(1)}, bf16[272,1024]{1,0:T(8,128)(2,1)S(1)}, u32[]{:S(2)}, u32[]{:S(2)}) collective-permute-start(bf16[272,1024]{1,0:T(8,128)(2,1)S(1)} %constant_dynamic-update-slice_fusion), channel_id=1, source_target_pairs={{0,1},{1,0},{2,3},{3,2},{4,5},{5,4},{6,7},{7,6},{8,9},{9,8},{10,11... | collective-permute-start | bytes 1671176 | tf_op jit(solution)/shard_map/ppermute | solution.py:65
  110.6 10.4 %collective-permute-start.13 = (bf16[128,1024]{1,0:T(8,128)(2,1)S(1)}, bf16[128,1024]{1,0:T(8,128)(2,1)S(1)}, u32[]{:S(2)}, u32[]{:S(2)}) collective-permute-start(bf16[128,1024]{1,0:T(8,128)(2,1)S(1)} %slice.130), channel_id=1, source_target_pairs={{0,2},{1,3},{2,4},{3,5},{4,6},{5,7},{6,0},{7,1},{8,10},{9,11},{10,... | collective-permute-start | bytes 786440 | tf_op jit(solution)/shard_map/ppermute | solution.py:70
  114.5 10.6 %collective-permute-start.14 = (bf16[128,1024]{1,0:T(8,128)(2,1)S(1)}, bf16[128,1024]{1,0:T(8,128)(2,1)S(1)}, u32[]{:S(2)}, u32[]{:S(2)}) collective-permute-start(bf16[128,1024]{1,0:T(8,128)(2,1)S(1)} %slice.131), channel_id=1, source_target_pairs={{0,6},{1,7},{2,0},{3,1},{4,2},{5,3},{6,4},{7,5},{8,14},{9,15},{10,... | collective-permute-start | bytes 786440 | tf_op jit(solution)/shard_map/ppermute | solution.py:70
  117.4 10.3 %collective-permute-start.10 = (bf16[256,1024]{1,0:T(8,128)(2,1)S(1)}, bf16[256,1024]{1,0:T(8,128)(2,1)S(1)}, u32[]{:S(2)}, u32[]{:S(2)}) collective-permute-start(bf16[256,1024]{1,0:T(8,128)(2,1)S(1)} %collective-permute-done.8), channel_id=1, source_target_pairs={{0,1},{1,0},{2,3},{3,2},{4,5},{5,4},{6,7},{7,6},{8,9},{9,8},{10,11... | collective-permute-start | bytes 1572872 | tf_op jit(solution)/shard_map/ppermute | solution.py:65
  121.1 7.0 %collective-permute-start.6 = (bf16[256,1024]{1,0:T(8,128)(2,1)S(1)}, bf16[256,1024]{1,0:T(8,128)(2,1)S(1)}, u32[]{:S(2)}, u32[]{:S(2)}) collective-permute-start(bf16[256,1024]{1,0:T(8,128)(2,1)S(1)} %collective-permute-done.4), channel_id=1, source_target_pairs={{0,1},{1,0},{2,3},{3,2},{4,5},{5,4},{6,7},{7,6},{8,9},{9,8},{10,11... | collective-permute-start | bytes 1572872 | tf_op jit(solution)/shard_map/ppermute | solution.py:65
  125.2 3.8 %collective-permute-start.16 = (bf16[256,1024]{1,0:T(8,128)(2,1)S(1)}, bf16[256,1024]{1,0:T(8,128)(2,1)S(1)}, u32[]{:S(2)}, u32[]{:S(2)}) collective-permute-start(bf16[256,1024]{1,0:T(8,128)(2,1)S(1)} %pad_maximum_fusion.9), channel_id=1, source_target_pairs={{0,1},{1,0},{2,3},{3,2},{4,5},{5,4},{6,7},{7,6},{8,9},{9,8},{10,11... | collective-permute-start | bytes 1572872 | tf_op jit(solution)/shard_map/ppermute | solution.py:65
  198.1 6.2 %collective-permute-start.18 = (bf16[2,128,1,128]{3,1,0,2:T(8,128)(2,1)S(1)}, bf16[2,128,1,128]{3,1,0,2:T(8,128)(2,1)S(1)}, u32[]{:S(2)}, u32[]{:S(2)}) collective-permute-start(bf16[2,128,1,128]{3,1,0,2:T(8,128)(2,1)S(1)} %slice.142), channel_id=1, source_target_pairs={{0,256},{256,0},{1,257},{257,1},{2,258},{258,2},{3,259},{259,3},{4... | collective-permute-start | bytes 196616 | tf_op jit(solution)/shard_map/ppermute | solution.py:60
  205.9 140.1 %all-to-all-start.1 = ((bf16[32,2,2,8,128]{4,3,2,1,0:T(8,128)(2,1)}), bf16[32,2,2,8,128]{4,3,2,1,0:T(8,128)(2,1)S(1)}, u32[]{:S(2)}, u32[]{:S(2)}) async-start(bf16[32,2,2,8,128]{4,3,2,1,0:T(8,128)(2,1)} %broadcast_select_fusion), calls=%async_computation.1 | async-start | bytes 524288 | tf_op jit(solution)/shard_map/all_to_all | solution.py:214
  342.7 6.9 %collective-permute-start.19 = (bf16[2,128,2,128]{3,1,2,0:T(8,128)(2,1)S(1)}, bf16[2,128,2,128]{3,1,2,0:T(8,128)(2,1)S(1)}, u32[]{:S(2)}, u32[]{:S(2)}) collective-permute-start(bf16[2,128,2,128]{3,1,2,0:T(8,128)(2,1)S(1)} %pad_maximum_fusion.10), channel_id=1, source_target_pairs={{0,256},{256,0},{1,257},{257,1},{2,258},{258,2},{3,259},{259,3},{4... | collective-permute-start | bytes 393224 | tf_op jit(solution)/shard_map/ppermute | solution.py:60
Sparse Core Ops, SparseCore 0:
  10.7 179.5 all-gather.5
  193.0 141.5 all-gather.3
